TPU v7x, 32 devices: a whole 2x2x4 slice. The times are simulated.
32 devices in a mesh: items: 4 (over y, x), users: 8 (over z, core).
Axes of the slice: x: 2, y: 2, z: 4, core: 2. Of those that a mesh axis runs over, the one named last changes fastest.
Arguments:
- capsules: bfloat16 [512, 8, 128], P('users'), may hold values from -6 to 6
- bank: bfloat16 [32768, 128], P(('items', 'users')), may hold values from -0.5 to 0.5
Outputs:
- relative: float32 [512, 32], P('users', 'items')
- peak: float32 [512], P('users')
All inputs are finite; a program needn't handle non-finite values.
Results may differ from a plain program's by a relative error of at most 0.0003.
Values may be sent and summed in bfloat16 or wider, within the bound.
A program may use at most 64 MiB of HBM per device.

v0:
```python
import jax
import jax.numpy as jnp
from jax import lax
from jax.sharding import PartitionSpec as P

BLOCK = 1024


def block_peaks(caps, rows):
    users_here = caps.shape[0]
    flat = caps.reshape(users_here * caps.shape[1], caps.shape[2])
    count = rows.shape[0] // BLOCK
    blocks = rows.reshape(count, BLOCK, rows.shape[1])

    def one_block(item_rows):
        score = lax.dot_general(
            flat, item_rows, (((1,), (1,)), ((), ())), preferred_element_type=jnp.float32
        )
        return jnp.max(score.reshape(users_here, -1), axis=1)

    return lax.map(one_block, blocks).T


def per_device(capsules, bank):
    everyone = lax.all_gather(capsules, "users", axis=0, tiled=True)
    own_block = block_peaks(everyone, bank)
    table = lax.all_to_all(own_block, "users", split_axis=0, concat_axis=1, tiled=True)
    peak = lax.pmax(jnp.max(table, axis=1), "items")
    return (table - peak[:, None], peak)


def solution(mesh):
    return jax.shard_map(
        per_device,
        mesh=mesh,
        in_specs=(P("users", None, None), P(("items", "users"), None)),
        out_specs=(P("users", "items"), P("users")),
        check_vma=False,
    )
```

profile of v0, /device:TPU:0, one launch (start us, length us, event | category | flops | bytes accessed | tf_op | source)
XLA Modules:
  0.0 64.6 jit_solution(8044447022359275363)
XLA Ops:
  7.2 0.0 copy-start
  7.2 0.0 all-gather.2.cloned.1.call-start
  7.2 0.7 %all-gather.2.cloned.1.call-update = ((bf16[64,8,128]{2,1,0:T(8,128)(2,1)}), bf16[512,8,128]{2,1,0:T(8,128)(2,1)}) async-update(((), (), s32[]{:S(2)}) %all-gather.2.cloned.1.call-start, bf16[64,8,128]{2,1,0:T(8,128)(2,1)} %param.2) | async-update | bytes 1310744
  7.9 26.7 %all-gather.2.cloned.1.call-done = bf16[512,8,128]{2,1,0:T(8,128)(2,1)} async-done(((bf16[64,8,128]{2,1,0:T(8,128)(2,1)}), bf16[512,8,128]{2,1,0:T(8,128)(2,1)}) %all-gather.2.cloned.1.call-update) | async-done | bytes 1048592 | tf_op jit(solution)/shard_map/all_gather | solution.py:25
  34.6 0.0 copy-done
  34.6 3.6 %convolution_reduce_fusion = f32[4096]{0:T(1024)S(1)} fusion(bf16[1024,128]{1,0:T(8,128)(2,1)S(1)} %copy-done, bf16[512,8,128]{2,1,0:T(8,128)(2,1)} %all-gather.2.cloned.1.call-done), kind=kOutput, calls=%fused_computation | convolution fusion | flops 1077932032 | bytes 1327104 | tf_op jit(solution)/shard_map/while/body/eval_jaxpr/dot_general | solution.py:16
  38.2 0.2 reduce_max.27
  38.3 0.1 reduce_max.28
  38.5 0.1 all_to_all.14
  38.6 8.8 %all_to_all.19 = f32[8,64,1]{1,2,0:T(1,128)S(1)} all-to-all(f32[8,64,1]{1,2,0:T(1,128)S(1)} %all_to_all.14), channel_id=1, replica_groups=mesh['items'=4,'users'=8] {'users'}, dimensions={0} | all-to-all | bytes 4096 | tf_op jit(solution)/shard_map/all_to_all | solution.py:27
  47.3 9.8 %pmax.7 = f32[64]{0:T(128)S(1)} all-reduce(f32[64]{0:T(128)S(1)} %reduce_max.29), channel_id=1, replica_groups=mesh['items'=4,'users'=8] {'items'}, use_global_device_ids=true, to_apply=%region_3.4 | all-reduce | flops 64 | bytes 512 | tf_op jit(solution)/shard_map/pmax | solution.py:28
  57.1 0.0 copy-start.1
  57.1 0.6 broadcast_subtract_fusion
  57.7 0.0 copy-done.1
  (1 shorter events, 0.0 us)
Async XLA Ops:
  7.2 27.4 %copy-start = (bf16[1024,128]{1,0:T(8,128)(2,1)S(1)}, bf16[1024,128]{1,0:T(8,128)(2,1)}, u32[]{:S(2)}) copy-start(bf16[1024,128]{1,0:T(8,128)(2,1)} %param.3) | copy-start | bytes 786436
  7.2 27.4 %all-gather.2.cloned.1.call-start = ((), (), s32[]{:S(2)}) async-start(), calls=%async_computation.1 | async-start | bytes 1179648 | tf_op jit(solution)/shard_map/all_gather | solution.py:25
  57.1 0.6 copy-start.1
Sparse Core Ops, SparseCore 0:
  9.6 24.9 all-gather.1
where the time goes:
time: 64.8 us; the launch traced here: 64.6 us
  waiting for transfers between devices  27.3 us (42%)
  blocking collectives  18.5 us (29%)
  between operations  14.1 us (22%)
  matrix products  3.58 us (6%)
  other arithmetic  0.77 us (1%)
    all_gather x1, waiting for transfers between devices, per_device(): everyone = lax.all_gather(capsules, 'users', axis=0, tiled=True)  26.7 us
    pmax x1, blocking collectives, per_device(): peak = lax.pmax(jnp.max(table, axis=1), 'items')  9.77 us
    all_to_all x1, blocking collectives, per_device(): lax.all_to_all(own_block, 'users', split_axis=0, concat_axis=1, tiled=True)  8.75 us
    dot_general x1, matrix products, one_block(): lax.dot_general(flat, item_rows, (((1,), (1,)), ((), ())), preferred_elem...  3.58 us
  transfers between devices with their start and end apart: 1, of which 1 were waited for; matrix products, arithmetic and copies ran while one was open for 0% of the time, Pallas kernels for 0%

commit v1 on v0

v1 whole, which is shorter than its diff:
```python
import functools

import jax
import jax.numpy as jnp
from jax import lax
from jax.experimental import pallas as pl
from jax.experimental.pallas import tpu as pltpu
from jax.sharding import PartitionSpec as P

BLOCK = 1024
LANES = 128
MESH = pl.DeviceIdType.MESH


def landed(ref, sem):
    pltpu.make_async_copy(ref, ref, sem).wait()


def partner_line(z, d, count):
    if count & (count - 1):
        return (z + d) % count
    out, bit = 0, 1
    while bit < count:
        out = out + ((z // bit + d // bit) % 2) * bit
        bit *= 2
    return out


def fold_capsules(acc):
    tiles = acc.shape[1] // LANES
    lane = lax.broadcasted_iota(jnp.int32, (8, LANES), 1) % 8
    out = None
    for t in range(tiles):
        v = acc[:, t * LANES : (t + 1) * LANES]
        for shift in (1, 2, 4):
            v = jnp.maximum(v, pltpu.roll(v, LANES - shift, 1))
        v = v if t == 0 else pltpu.roll(v, t, 1)
        out = v if out is None else jnp.where(lane == t, v, out)
    return jnp.max(out, axis=0, keepdims=True)


def kernel(
    items, users, caps_hbm, bank_hbm, rel_ref, peak_ref,
    own, bank, all_caps, res, table,
    load_sem, send_sem, recv_sem, back_send, back_recv,
):
    i = lax.axis_index("items")
    g = lax.axis_index("users")
    chips = users // 2
    z, c = g // 2, g % 2
    p = 2 * z + 1 - c
    pieces, rows = all_caps.shape[1], all_caps.shape[2]

    load_caps = pltpu.make_async_copy(caps_hbm, own, load_sem.at[0])
    load_caps.start()
    load_bank = pltpu.make_async_copy(bank_hbm, bank, load_sem.at[1])
    load_bank.start()

    barrier = pltpu.get_barrier_semaphore()

    def hello(jj, gg):
        pl.semaphore_signal(
            barrier, inc=1, device_id={"items": jj, "users": gg}, device_id_type=MESH
        )

    def hello_line(d, carry):
        hello(i, 2 * partner_line(z, d, chips) + c)
        return carry

    lax.fori_loop(1, chips, hello_line, 0, unroll=chips <= 8)
    for d in range(1, items):
        hello((i + d) % items, g)
    hello(i, p)
    pl.semaphore_wait(barrier, chips - 1 + items - 1 + 1)
    load_caps.wait()

    def send(src, dst, recv, jj, gg):
        pltpu.make_async_remote_copy(
            src_ref=src, dst_ref=dst, send_sem=send_sem.at[0], recv_sem=recv,
            device_id={"items": jj, "users": gg}, device_id_type=MESH,
        ).start()

    def send_line(d, carry):
        far = partner_line(z, chips - d, chips)
        send(own.at[i], all_caps.at[g, i], recv_sem.at[g, i], i, 2 * far + c)
        return carry

    lax.fori_loop(1, chips, send_line, 0, unroll=chips <= 8)
    send(own, all_caps.at[g], recv_sem.at[g, 0], i, p)
    load_bank.wait()

    def block_peak(group):
        score = lax.dot_general(
            bank[...], group.reshape(pieces * rows, group.shape[-1]),
            (((1,), (1,)), ((), ())), preferred_element_type=jnp.float32,
        )
        acc = jnp.max(score.reshape(-1, 8, pieces * rows), axis=0)
        return fold_capsules(acc)

    def answer(gg, jj):
        row = ((i - jj + items) % items) * users + g
        pltpu.make_async_remote_copy(
            src_ref=res.at[gg], dst_ref=table.at[row],
            send_sem=back_send.at[0], recv_sem=back_recv.at[0],
            device_id={"items": jj, "users": gg}, device_id_type=MESH,
        ).start()

    table[g] = block_peak(own[...])
    res[g] = table[g]

    def relay(d, carry):
        from_g = 2 * partner_line(z, d, chips) + c
        piece, sem = all_caps.at[from_g, i], recv_sem.at[from_g, i]
        landed(piece, sem)
        for s in range(1, items):
            send(piece, piece, sem, (i + s) % items, g)
        send(piece, piece, sem, i, p)
        return carry

    lax.fori_loop(1, chips, relay, 0, unroll=chips <= 8)
    landed(all_caps.at[p], recv_sem.at[p, 0])
    res[p] = block_peak(all_caps[p])

    def same_core(d, carry):
        from_g = 2 * partner_line(z, d, chips) + c
        for s in range(1, items):
            q = (i + s) % items
            piece, sem = all_caps.at[from_g, q], recv_sem.at[from_g, q]
            landed(piece, sem)
            send(piece, piece, sem, i, p)
        res[from_g] = block_peak(all_caps[from_g])
        for s in range(items):
            answer(from_g, (i + s) % items)
        return carry

    lax.fori_loop(1, chips, same_core, 0)

    def other_core(d, carry):
        from_g = 2 * partner_line(z, d, chips) + 1 - c
        for q in range(items):
            landed(all_caps.at[from_g, q], recv_sem.at[from_g, q])
        res[from_g] = block_peak(all_caps[from_g])
        for s in range(items):
            answer(from_g, (i + s) % items)
        return carry

    lax.fori_loop(1, chips, other_core, 0)
    for s in range(items):
        answer(p, (i + s) % items)
    for s in range(1, items):
        answer(g, (i + s) % items)

    blocks = items * users
    landed(table.at[pl.ds(0, blocks - 1)], back_recv.at[0])
    peak = jnp.max(table[...], axis=0)
    both = jnp.concatenate([table[:users].reshape(users, LANES) - peak, peak], axis=0)
    tiles = pieces * rows // LANES
    spread = LANES // 8
    lane = lax.broadcasted_iota(jnp.int32, both.shape, 1)
    pick = (lane % spread) * 8 + lane // spread
    both = jnp.take_along_axis(both, pick, axis=1)
    rel_ref[...] = both[:users, : tiles * spread]
    peak_ref[...] = both[users:, : tiles * spread]

    landed(all_caps.at[pl.ds(0, users - 1)], send_sem.at[0])
    landed(table.at[pl.ds(0, blocks - 1)], back_send.at[0])


def per_device(items, users, capsules, bank):
    users_here, k, width = capsules.shape
    assert k == 8 and bank.shape[0] == BLOCK and users_here * k <= 8 * LANES
    rows = users_here * k // items
    blocks = items * users
    relative, peak = pl.pallas_call(
        functools.partial(kernel, items, users),
        out_shape=(
            jax.ShapeDtypeStruct((users, users_here), jnp.float32),
            jax.ShapeDtypeStruct((1, users_here), jnp.float32),
        ),
        in_specs=[pl.BlockSpec(memory_space=pl.ANY)] * 2,
        out_specs=(pl.BlockSpec(memory_space=pltpu.VMEM),) * 2,
        scratch_shapes=[
            pltpu.VMEM((items, rows, width), capsules.dtype),
            pltpu.VMEM(bank.shape, bank.dtype),
            pltpu.VMEM((users, items, rows, width), capsules.dtype),
            pltpu.VMEM((users, 1, LANES), jnp.float32),
            pltpu.VMEM((blocks, 1, LANES), jnp.float32),
            pltpu.SemaphoreType.DMA((2,)),
            pltpu.SemaphoreType.DMA((1,)),
            pltpu.SemaphoreType.DMA((users, items)),
            pltpu.SemaphoreType.DMA((1,)),
            pltpu.SemaphoreType.DMA((1,)),
        ],
        compiler_params=pltpu.CompilerParams(
            collective_id=0, has_side_effects=True, vmem_limit_bytes=60 * 2**20
        ),
    )(capsules.reshape(items, rows, width), bank)
    return relative.T, peak.reshape(users_here)


def solution(mesh):
    return jax.shard_map(
        functools.partial(per_device, mesh.shape["items"], mesh.shape["users"]),
        mesh=mesh,
        in_specs=(P("users", None, None), P(("items", "users"), None)),
        out_specs=(P("users", "items"), P("users")),
        check_vma=False,
    )
```

time: 64.8 us -> 24.4 us (0.38)
  waiting for transfers between devices: 27.3 us -> 0 us
  Pallas kernels: 0 us -> 21.5 us
  blocking collectives: 18.5 us -> 0 us
  between operations: 14.1 us -> 0.65 us
  matrix products: 3.58 us -> 0 us
  local copies, waits for them, and re-layouts: 0.25 us -> 1.82 us
  other arithmetic: 0.77 us -> 0 us
    all_gather x1 -> x0, waiting for transfers between devices: 26.7 us -> none  [per_device(): everyone = lax.all_gather(capsules, 'users', axis=0, tiled=True)]
    pallas_call x0 -> x1, Pallas kernels: none -> 21.5 us  [per_device(): pl.pallas_call(functools.partial(kernel, items, users), out_shape=(jax.Sh...]
    pmax x1 -> x0, blocking collectives: 9.77 us -> none  [per_device(): peak = lax.pmax(jnp.max(table, axis=1), 'items')]
    all_to_all x1 -> x0, blocking collectives: 8.75 us -> none  [per_device(): lax.all_to_all(own_block, 'users', split_axis=0, concat_axis=1, tiled=True)]
    dot_general x1 -> x0, matrix products: 3.58 us -> none  [one_block(): lax.dot_general(flat, item_rows, (((1,), (1,)), ((), ())), preferred_elem...]
    unnamed x4 -> x6, local copies, waits for them, and re-layouts: 0.01 us -> 1.82 us
    unnamed x1 -> x0, waiting for transfers between devices: 0.68 us -> none
  transfers between devices with their start and end apart: 1 -> 0, of which waited for: 1 -> 0; matrix products, arithmetic and copies ran while one was open for 0% -> 0% of each run, Pallas kernels for 0% -> 0%
where the time goes in v1:
time: 24.4 us; the launch traced here: 24 us
  Pallas kernels  21.5 us (88%)
  local copies, waits for them, and re-layouts  1.82 us (7%)
  between operations  0.65 us (3%)
    pallas_call x1, Pallas kernels, per_device(): pl.pallas_call(functools.partial(kernel, items, users), out_shape=(jax.Sh...  21.5 us
    unnamed x6, local copies, waits for them, and re-layouts  1.82 us

profile of v1, /device:TPU:0, one launch (start us, length us, event | category | flops | bytes accessed | tf_op | source)
XLA Modules:
  0.0 24.0 jit_solution(16726152973874555812)
XLA Ops:
  0.6 21.5 %shard_map.41 = (f32[8,64]{1,0:T(8,128)}, f32[1,64]{1,0:T(1,128)}) custom-call(bf16[4,128,128]{2,1,0:T(8,128)(2,1)} %bitcast.3, bf16[1024,128]{1,0:T(8,128)(2,1)} %bank_hbm.1), custom_call_target="tpu_custom_call" | custom-call | tf_op jit(solution)/shard_map/pallas_call | solution.py:174
  22.1 0.0 copy-start
  22.1 0.7 %copy-done = f32[8,64]{1,0:T(8,128)S(1)} copy-done((f32[8,64]{1,0:T(8,128)S(1)}, f32[8,64]{1,0:T(8,128)}, u32[]{:S(2)}) %copy-start) | copy-done | bytes 2072
  22.8 0.0 copy-start.1
  22.8 0.6 %copy.6 = f32[64,8]{0,1:T(8,128)} copy(f32[64,8]{0,1:T(8,128)S(1)} %bitcast.4) | data formatting | bytes 4096
  23.4 0.0 copy-done.1
  23.4 0.5 %copy.7 = f32[64]{0:T(128)} copy(f32[64]{0:T(128)S(1)} %bitcast.5) | data formatting | bytes 512
Async XLA Ops:
  22.1 0.7 %copy-start = (f32[8,64]{1,0:T(8,128)S(1)}, f32[8,64]{1,0:T(8,128)}, u32[]{:S(2)}) copy-start(f32[8,64]{1,0:T(8,128)} %get-tuple-element.4) | copy-start | bytes 6148
  22.8 0.6 %copy-start.1 = (f32[1,64]{1,0:T(1,128)S(1)}, f32[1,64]{1,0:T(1,128)}, u32[]{:S(2)}) copy-start(f32[1,64]{1,0:T(1,128)} %get-tuple-element.5) | copy-start | bytes 772

commit v2 on v1

--- a/solution.py
+++ b/solution.py
@@ -26,17 +26,17 @@
     return out
 
 
-def fold_capsules(acc):
-    tiles = acc.shape[1] // LANES
-    lane = lax.broadcasted_iota(jnp.int32, (8, LANES), 1) % 8
+def by_user(top):
+    spread = LANES // 8
+    lane = lax.broadcasted_iota(jnp.int32, (top.shape[0], LANES), 1)
     out = None
-    for t in range(tiles):
-        v = acc[:, t * LANES : (t + 1) * LANES]
+    for t in range(top.shape[1] // LANES):
+        v = top[:, t * LANES : (t + 1) * LANES]
         for shift in (1, 2, 4):
             v = jnp.maximum(v, pltpu.roll(v, LANES - shift, 1))
-        v = v if t == 0 else pltpu.roll(v, t, 1)
-        out = v if out is None else jnp.where(lane == t, v, out)
-    return jnp.max(out, axis=0, keepdims=True)
+        v = jnp.take_along_axis(v, (lane % spread) * 8, axis=1)
+        out = v if out is None else jnp.where(lane // spread == t, v, out)
+    return out
 
 
 def kernel(
@@ -94,8 +94,7 @@
             bank[...], group.reshape(pieces * rows, group.shape[-1]),
             (((1,), (1,)), ((), ())), preferred_element_type=jnp.float32,
         )
-        acc = jnp.max(score.reshape(-1, 8, pieces * rows), axis=0)
-        return fold_capsules(acc)
+        return jnp.max(score, axis=0, keepdims=True)
 
     def answer(gg, jj):
         row = ((i - jj + items) % items) * users + g
@@ -152,15 +151,11 @@
 
     blocks = items * users
     landed(table.at[pl.ds(0, blocks - 1)], back_recv.at[0])
-    peak = jnp.max(table[...], axis=0)
-    both = jnp.concatenate([table[:users].reshape(users, LANES) - peak, peak], axis=0)
-    tiles = pieces * rows // LANES
-    spread = LANES // 8
-    lane = lax.broadcasted_iota(jnp.int32, both.shape, 1)
-    pick = (lane % spread) * 8 + lane // spread
-    both = jnp.take_along_axis(both, pick, axis=1)
-    rel_ref[...] = both[:users, : tiles * spread]
-    peak_ref[...] = both[users:, : tiles * spread]
+    best = jnp.max(table[...], axis=0)
+    near = table[:users].reshape(users, best.shape[1])
+    both = by_user(jnp.concatenate([near, best], axis=0))[:, : peak_ref.shape[1]]
+    rel_ref[...] = both[:users] - both[users:]
+    peak_ref[...] = both[users:]
 
     landed(all_caps.at[pl.ds(0, users - 1)], send_sem.at[0])
     landed(table.at[pl.ds(0, blocks - 1)], back_send.at[0])
@@ -174,17 +169,17 @@
     relative, peak = pl.pallas_call(
         functools.partial(kernel, items, users),
         out_shape=(
-            jax.ShapeDtypeStruct((users, users_here), jnp.float32),
-            jax.ShapeDtypeStruct((1, users_here), jnp.float32),
+            pltpu.VMEM((users, users_here), jnp.float32),
+            pltpu.VMEM((1, users_here), jnp.float32),
         ),
-        in_specs=[pl.BlockSpec(memory_space=pl.ANY)] * 2,
+        in_specs=[pl.BlockSpec(memory_space=pltpu.HBM)] * 2,
         out_specs=(pl.BlockSpec(memory_space=pltpu.VMEM),) * 2,
         scratch_shapes=[
             pltpu.VMEM((items, rows, width), capsules.dtype),
             pltpu.VMEM(bank.shape, bank.dtype),
             pltpu.VMEM((users, items, rows, width), capsules.dtype),
-            pltpu.VMEM((users, 1, LANES), jnp.float32),
-            pltpu.VMEM((blocks, 1, LANES), jnp.float32),
+            pltpu.VMEM((users, 1, users_here * k), jnp.float32),
+            pltpu.VMEM((blocks, 1, users_here * k), jnp.float32),
             pltpu.SemaphoreType.DMA((2,)),
             pltpu.SemaphoreType.DMA((1,)),
             pltpu.SemaphoreType.DMA((users, items)),

time: 24.4 us -> 22.3 us (0.914)
  Pallas kernels: 21.5 us -> 20.3 us
  local copies, waits for them, and re-layouts: 1.82 us -> 1.11 us
    pallas_call x1, Pallas kernels: 21.5 us -> 20.3 us  [per_device(): pl.pallas_call(functools.partial(kernel, items, users), out_shape=(pltpu....]
    unnamed x6 -> x2, local copies, waits for them, and re-layouts: 1.82 us -> 1.11 us
where the time goes in v2:
time: 22.3 us; the launch traced here: 22 us
  Pallas kernels  20.3 us (91%)
  local copies, waits for them, and re-layouts  1.11 us (5%)
  between operations  0.64 us (3%)
    pallas_call x1, Pallas kernels, per_device(): pl.pallas_call(functools.partial(kernel, items, users), out_shape=(pltpu....  20.3 us
    unnamed x2, local copies, waits for them, and re-layouts  1.11 us

profile of v2, /device:TPU:0, one launch (start us, length us, event | category | flops | bytes accessed | tf_op | source)
XLA Modules:
  0.0 22.0 jit_solution(16392180185704477943)
XLA Ops:
  0.6 20.3 %shard_map.41 = (f32[8,64]{1,0:T(8,128)S(1)}, f32[1,64]{1,0:T(1,128)S(1)}) custom-call(bf16[4,128,128]{2,1,0:T(8,128)(2,1)} %bitcast.5, bf16[1024,128]{1,0:T(8,128)(2,1)} %bank_hbm.1), custom_call_target="tpu_custom_call" | custom-call | tf_op jit(solution)/shard_map/pallas_call | solution.py:169
  20.9 0.6 %copy.6 = f32[64,8]{0,1:T(8,128)} copy(f32[64,8]{0,1:T(8,128)S(1)} %bitcast.3) | data formatting | bytes 4096
  21.5 0.5 %copy.7 = f32[64]{0:T(128)} copy(f32[64]{0:T(128)S(1)} %bitcast.4) | data formatting | bytes 512

commit v3 on v2

--- a/solution.py
+++ b/solution.py
@@ -16,7 +16,7 @@
     pltpu.make_async_copy(ref, ref, sem).wait()
 
 
-def partner_line(z, d, count):
+def peer(z, d, count):
     if count & (count - 1):
         return (z + d) % count
     out, bit = 0, 1
@@ -49,6 +49,7 @@
     chips = users // 2
     z, c = g // 2, g % 2
     p = 2 * z + 1 - c
+    opposite = peer(i, items - 1, items)
     pieces, rows = all_caps.shape[1], all_caps.shape[2]
 
     load_caps = pltpu.make_async_copy(caps_hbm, own, load_sem.at[0])
@@ -64,7 +65,7 @@
         )
 
     def hello_line(d, carry):
-        hello(i, 2 * partner_line(z, d, chips) + c)
+        hello(i, 2 * peer(z, d, chips) + c)
         return carry
 
     lax.fori_loop(1, chips, hello_line, 0, unroll=chips <= 8)
@@ -81,11 +82,15 @@
         ).start()
 
     def send_line(d, carry):
-        far = partner_line(z, chips - d, chips)
+        far = peer(z, chips - d, chips)
         send(own.at[i], all_caps.at[g, i], recv_sem.at[g, i], i, 2 * far + c)
         return carry
 
     lax.fori_loop(1, chips, send_line, 0, unroll=chips <= 8)
+    send(
+        own.at[opposite], all_caps.at[g, opposite], recv_sem.at[g, opposite],
+        i, 2 * peer(z, 1, chips) + c,
+    )
     send(own, all_caps.at[g], recv_sem.at[g, 0], i, p)
     load_bank.wait()
 
@@ -108,11 +113,12 @@
     res[g] = table[g]
 
     def relay(d, carry):
-        from_g = 2 * partner_line(z, d, chips) + c
+        from_g = 2 * peer(z, d, chips) + c
         piece, sem = all_caps.at[from_g, i], recv_sem.at[from_g, i]
         landed(piece, sem)
-        for s in range(1, items):
-            send(piece, piece, sem, (i + s) % items, g)
+        for s in range(1, items - 1):
+            send(piece, piece, sem, peer(i, s, items), g)
+        pl.when(d > 1)(lambda: send(piece, piece, sem, opposite, g))
         send(piece, piece, sem, i, p)
         return carry
 
@@ -121,7 +127,7 @@
     res[p] = block_peak(all_caps[p])
 
     def same_core(d, carry):
-        from_g = 2 * partner_line(z, d, chips) + c
+        from_g = 2 * peer(z, d, chips) + c
         for s in range(1, items):
             q = (i + s) % items
             piece, sem = all_caps.at[from_g, q], recv_sem.at[from_g, q]
@@ -132,10 +138,10 @@
             answer(from_g, (i + s) % items)
         return carry
 
-    lax.fori_loop(1, chips, same_core, 0)
+    lax.fori_loop(1, chips, same_core, 0, unroll=chips <= 8)
 
     def other_core(d, carry):
-        from_g = 2 * partner_line(z, d, chips) + 1 - c
+        from_g = 2 * peer(z, d, chips) + 1 - c
         for q in range(items):
             landed(all_caps.at[from_g, q], recv_sem.at[from_g, q])
         res[from_g] = block_peak(all_caps[from_g])
@@ -143,7 +149,7 @@
             answer(from_g, (i + s) % items)
         return carry
 
-    lax.fori_loop(1, chips, other_core, 0)
+    lax.fori_loop(1, chips, other_core, 0, unroll=chips <= 8)
     for s in range(items):
         answer(p, (i + s) % items)
     for s in range(1, items):
@@ -163,7 +169,7 @@
 
 def per_device(items, users, capsules, bank):
     users_here, k, width = capsules.shape
-    assert k == 8 and bank.shape[0] == BLOCK and users_here * k <= 8 * LANES
+    assert items & (items - 1) == 0 and users & (users - 1) == 0 and k == 8 and bank.shape[0] == BLOCK and users_here * k <= 8 * LANES
     rows = users_here * k // items
     blocks = items * users
     relative, peak = pl.pallas_call(

time: 22.3 us -> 21.8 us (0.978)
  Pallas kernels: 20.3 us -> 19.8 us
    pallas_call x1, Pallas kernels: 20.3 us -> 19.8 us  [per_device(): pl.pallas_call(functools.partial(kernel, items, users), out_shape=(pltpu....]
where the time goes in v3:
time: 21.8 us; the launch traced here: 21.5 us
  Pallas kernels  19.8 us (91%)
  local copies, waits for them, and re-layouts  1.11 us (5%)
  between operations  0.64 us (3%)
    pallas_call x1, Pallas kernels, per_device(): pl.pallas_call(functools.partial(kernel, items, users), out_shape=(pltpu....  19.8 us
    unnamed x2, local copies, waits for them, and re-layouts  1.11 us

profile of v3, /device:TPU:0, one launch (start us, length us, event | category | flops | bytes accessed | tf_op | source)
XLA Modules:
  0.0 21.5 jit_solution(6308720474547310602)
XLA Ops:
  0.6 19.8 %shard_map.41 = (f32[8,64]{1,0:T(8,128)S(1)}, f32[1,64]{1,0:T(1,128)S(1)}) custom-call(bf16[4,128,128]{2,1,0:T(8,128)(2,1)} %bitcast.5, bf16[1024,128]{1,0:T(8,128)(2,1)} %bank_hbm.1), custom_call_target="tpu_custom_call" | custom-call | tf_op jit(solution)/shard_map/pallas_call | solution.py:175
  20.4 0.6 %copy.6 = f32[64,8]{0,1:T(8,128)} copy(f32[64,8]{0,1:T(8,128)S(1)} %bitcast.3) | data formatting | bytes 4096
  21.0 0.5 %copy.7 = f32[64]{0:T(128)} copy(f32[64]{0:T(128)S(1)} %bitcast.4) | data formatting | bytes 512

commit v4 on v3

--- a/solution.py
+++ b/solution.py
@@ -165,6 +165,15 @@
 
     landed(all_caps.at[pl.ds(0, users - 1)], send_sem.at[0])
     landed(table.at[pl.ds(0, blocks - 1)], back_send.at[0])
+
+
+def put(relative, peak, relative_hbm, peak_hbm, sem):
+    first = pltpu.make_async_copy(relative, relative_hbm, sem.at[0])
+    second = pltpu.make_async_copy(peak, peak_hbm, sem.at[1])
+    first.start()
+    second.start()
+    first.wait()
+    second.wait()
 
 
 def per_device(items, users, capsules, bank):
@@ -196,6 +205,16 @@
             collective_id=0, has_side_effects=True, vmem_limit_bytes=60 * 2**20
         ),
     )(capsules.reshape(items, rows, width), bank)
+    relative, peak = pl.pallas_call(
+        put,
+        out_shape=(pltpu.HBM(relative.shape, relative.dtype), pltpu.HBM(peak.shape, peak.dtype)),
+        in_specs=[pl.BlockSpec(memory_space=pltpu.VMEM)] * 2,
+        out_specs=(pl.BlockSpec(memory_space=pltpu.HBM),) * 2,
+        scratch_shapes=[pltpu.SemaphoreType.DMA((2,))],
+    )(
+        pltpu.with_memory_space_constraint(relative, pltpu.VMEM),
+        pltpu.with_memory_space_constraint(peak, pltpu.VMEM),
+    )
     return relative.T, peak.reshape(users_here)
 
 

time: 21.8 us -> 21.3 us (0.977)
  local copies, waits for them, and re-layouts: 1.11 us -> 0 us
  Pallas kernels: 19.8 us -> 20.4 us
    unnamed x2 -> x0, local copies, waits for them, and re-layouts: 1.11 us -> none
    pallas_call x0 -> x1, Pallas kernels: none -> 0.61 us  [per_device(): pl.pallas_call(put, out_shape=(pltpu.HBM(relative.shape, relative.dtype),...]
where the time goes in v4:
time: 21.3 us; the launch traced here: 21 us
  Pallas kernels  20.4 us (96%)
  between operations  0.64 us (3%)
    pallas_call x1, Pallas kernels, per_device(): pl.pallas_call(functools.partial(kernel, items, users), out_shape=(pltpu....  19.8 us
    pallas_call x1, Pallas kernels, per_device(): pl.pallas_call(put, out_shape=(pltpu.HBM(relative.shape, relative.dtype),...  0.61 us

profile of v4, /device:TPU:0, one launch (start us, length us, event | category | flops | bytes accessed | tf_op | source)
XLA Modules:
  0.0 21.0 jit_solution(6681113477297365856)
XLA Ops:
  0.6 19.8 %shard_map.41 = (f32[8,64]{1,0:T(8,128)S(1)}, f32[1,64]{1,0:T(1,128)S(1)}) custom-call(bf16[4,128,128]{2,1,0:T(8,128)(2,1)} %bitcast.3, bf16[1024,128]{1,0:T(8,128)(2,1)} %bank_hbm.1), custom_call_target="tpu_custom_call" | custom-call | tf_op jit(solution)/shard_map/pallas_call | solution.py:184
  20.4 0.6 %shard_map.42 = (f32[8,64]{1,0:T(8,128)}, f32[1,64]{1,0:T(1,128)}) custom-call(f32[8,64]{1,0:T(8,128)S(1)} %get-tuple-element.6.relative, f32[1,64]{1,0:T(1,128)S(1)} %get-tuple-element.7.peak), custom_call_target="tpu_custom_call" | custom-call | tf_op jit(solution)/shard_map/pallas_call | solution.py:208
